TPU v7x, 16 devices: a 4x2x1 block of a 4x4x8 slice. The times are simulated.
16 devices in a mesh: dp: 2 (over y, z), sp: 8 (over x, core).
Axes of the slice: x: 4, y: 2, z: 1, core: 2. Of those that a mesh axis runs over, the one named last changes fastest.
The devices are a block of a 4x4x8 slice.
Arguments:
- q: bfloat16 [64, 48, 128], P('dp'), parts along dimension 0
- k: bfloat16 [64, 8192, 4, 128], P('dp', 'sp'), parts along dimension 0
- v: bfloat16 [64, 8192, 4, 128], P('dp', 'sp'), parts along dimension 0
Outputs:
- q: bfloat16 [64, 48, 128], P('dp'), parts along dimension 0
There are 2 independent parts. A program takes and returns all parts, laid end to end along the dimension named above; each array names one.
All inputs are finite; a program needn't handle non-finite values.
Results may differ from a plain program's by a relative error of at most 0.012.
Values are sent between devices in bfloat16 or wider.
A program may use at most 768 MiB of HBM per device.

v0:
```python
import jax
import jax.numpy as jnp
from jax import lax
from jax.sharding import PartitionSpec as P


def einsum(form, a, b):
    return jnp.einsum(form, a.astype(jnp.float32), b.astype(jnp.float32))


def part_of(q, k, v):
    grouped = q.reshape(q.shape[0], k.shape[2], -1, q.shape[2])
    scores = einsum("bgsd,bugd->bgsu", grouped, k) * q.shape[2] ** -0.5
    high = jnp.max(scores, -1, keepdims=True)
    weights = jnp.exp(scores - high)
    seen = einsum("bgsu,bugd->bgsd", weights.astype(jnp.bfloat16), v)
    return jnp.concatenate([seen, jnp.sum(weights, -1, keepdims=True), high], -1)


def together(parts):
    seen, total, high = parts[..., :-2], parts[..., -2:-1], parts[..., -1:]
    scale = jnp.exp(high - jnp.max(high, 0))
    return (jnp.sum(seen * scale, 0) / jnp.sum(total * scale, 0)).astype(jnp.bfloat16)


def solution(mesh):
    def step(q, k, v):
        return together(lax.all_gather(part_of(q, k, v), "sp")).reshape(q.shape)

    return jax.shard_map(
        step,
        mesh=mesh,
        in_specs=(P("dp", None, None), P("dp", "sp", None, None), P("dp", "sp", None, None)),
        out_specs=P("dp", None, None),
        check_vma=False,
    )
```

profile of v0, /device:TPU:113, one launch (start us, length us, event | category | flops | bytes accessed | tf_op | source)
XLA Modules:
  0.0 159.0 jit_solution(3305050129570740206)
XLA Ops:
  6.5 0.0 all-gather.3.cloned.1.call-start
  6.6 1.1 copy.30
  7.7 17.1 %multiply_reduce_fusion = (f32[32,4,12]{2,1,0:T(4,128)S(1)}, f32[32,4,12,1024]{3,2,1,0:T(8,128)S(1)}) fusion(bf16[32,1024,4,128]{3,2,1,0:T(4,128)(2,1)} %param.4, bf16[32,4,12,128]{3,0,2,1:T(8,128)(2,1)S(1)} %bitcast.13), kind=kOutput, calls=%fused_computation.5 | convolution fusion | flops 405797376 | bytes 40245248 | tf_op jit(solution)/shard_map/bgsd,bugd->bgsu/dot_general | solution.py:8
  24.8 0.0 copy-start.1
  24.8 3.2 %copy-done.1 = f32[32,4,12,1024]{3,2,1,0:T(8,128)} copy-done((f32[32,4,12,1024]{3,2,1,0:T(8,128)}, f32[32,4,12,1024]{3,2,1,0:T(8,128)S(1)}, u32[]{:S(2)}) %copy-start.1) | copy-done | bytes 6291480
  28.0 2.0 %fusion.4 = f32[32,4,12]{2,1,0:T(4,128)S(1)} fusion(f32[32,4,12,1024]{3,2,1,0:T(8,128)S(1)} %get-tuple-element.8, f32[32,4,12]{2,1,0:T(4,128)S(1)} %get-tuple-element.7), kind=kLoop, calls=%fused_computation.6 | loop fusion | flops 4717056 | bytes 6303744 | tf_op jit(solution)/shard_map/reduce_sum | solution.py:17
  30.0 18.9 %fusion = f32[32,4,12,128]{3,2,1,0:T(8,128)S(1)} fusion(bf16[32,1024,4,128]{3,2,1,0:T(4,128)(2,1)} %param.5, f32[32,4,12,1024]{3,2,1,0:T(8,128)} %copy-done.1, f32[32,4,12]{2,1,0:T(4,128)S(1)} %get-tuple-element.7), kind=kOutput, calls=%fused_computation | convolution fusion | flops 407371776 | bytes 40638464 | tf_op jit(solution)/shard_map/bgsu,bugd->bgsd/dot_general | solution.py:8
  48.9 0.9 copy.36
  49.8 0.9 copy.37
  50.7 0.4 pad_maximum_fusion
  51.1 2.5 %copy.38 = f32[32,4,12,130]{3,1,2,0:T(4,128)} copy(f32[32,4,12,130]{3,2,1,0:T(8,128)S(1)} %pad_maximum_fusion) | data formatting | bytes 1597440 | tf_op jit(solution)/shard_map/concatenate | solution.py:17
  53.6 0.1 all-gather.3.cloned.1.call-update
  53.7 66.7 %all-gather.3.cloned.1.call-done = f32[256,4,12,130]{3,1,2,0:T(4,128)} async-done(((f32[32,4,12,130]{3,1,2,0:T(4,128)}), f32[256,4,12,130]{3,1,2,0:T(4,128)}) %all-gather.3.cloned.1.call-update) | async-done | bytes 6389776 | tf_op jit(solution)/shard_map/all_gather | solution.py:28
  120.4 16.3 %copy.39 = f32[256,4,12,130]{3,0,2,1:T(8,128)} copy(f32[256,4,12,130]{3,1,2,0:T(4,128)} %all-gather.3.cloned.1.call-done) | data formatting | bytes 12779520 | tf_op jit(solution)/shard_map/all_gather | solution.py:28
  136.7 0.0 copy-start
  136.7 5.1 %slice_reduce_fusion = f32[32,4,12]{0,2,1:T(8,128)S(1)} fusion(f32[8,32,4,12,130]{4,1,0,3,2:T(8,128)} %bitcast.10), kind=kLoop, calls=%fused_computation.13 | loop fusion | flops 10752 | bytes 55296 | tf_op jit(solution)/shard_map/reduce_max | solution.py:22
  141.8 7.1 %fusion.6 = (f32[32,4,12]{0,2,1:T(8,128)S(1)}, f32[8,32,4,12]{1,0,3,2:T(8,128)S(1)}) fusion(f32[8,32,4,12,130]{4,1,0,3,2:T(8,128)} %bitcast.11, f32[32,4,12]{0,2,1:T(8,128)S(1)} %slice_reduce_fusion), kind=kLoop, calls=%fused_computation.9 | loop fusion | flops 35328 | bytes 159744 | tf_op jit(solution)/shard_map/reduce_sum | solution.py:23
  148.9 0.0 copy-done
  148.9 2.0 %fusion.7 = f32[32,4,12,128]{3,0,2,1:T(8,128)S(1)} fusion(f32[8,32,4,12,130]{4,1,0,3,2:T(8,128)S(1)} %bitcast.12, f32[8,32,4,12]{1,0,3,2:T(8,128)S(1)} %get-tuple-element.6), kind=kLoop, calls=%fused_computation.11 | loop fusion | flops 2949120 | bytes 7127040 | tf_op jit(solution)/shard_map/reduce_sum | solution.py:23
  151.0 0.3 fusion.12
  151.2 0.9 copy.42
  (1 shorter events, 0.0 us)
Async XLA Ops:
  6.5 113.9 %all-gather.3.cloned.1.call-start = ((), (), s32[]{:S(2)}) async-start(), calls=%async_computation | async-start | bytes 14155776 | tf_op jit(solution)/shard_map/all_gather | solution.py:28
  24.8 3.2 %copy-start.1 = (f32[32,4,12,1024]{3,2,1,0:T(8,128)}, f32[32,4,12,1024]{3,2,1,0:T(8,128)S(1)}, u32[]{:S(2)}) copy-start(f32[32,4,12,1024]{3,2,1,0:T(8,128)S(1)} %get-tuple-element.8) | copy-start | bytes 18874372
  136.7 12.2 %copy-start = (f32[256,4,12,130]{3,0,2,1:T(8,128)S(1)}, f32[256,4,12,130]{3,0,2,1:T(8,128)}, u32[]{:S(2)}) copy-start(f32[256,4,12,130]{3,0,2,1:T(8,128)} %copy.39) | copy-start | bytes 19169284
Sparse Core Ops, SparseCore 0:
  53.8 66.5 all-gather.2
where the time goes:
time: 159 us
  waiting for transfers between devices  66.8 us (42%)
  matrix products  36 us (23%)
  local copies, waits for them, and re-layouts  25.9 us (16%)
  other arithmetic  16.8 us (11%)
  between operations  13.5 us (8%)
    all_gather x1, waiting for transfers between devices, step(): return together(lax.all_gather(part_of(q, k, v), 'sp')).reshape(q.shape)  66.7 us
    dot_general x2, matrix products, einsum(): return jnp.einsum(form, a.astype(jnp.float32), b.astype(jnp.float32))  36 us
    all_gather x1, local copies, waits for them, and re-layouts, step(): return together(lax.all_gather(part_of(q, k, v), 'sp')).reshape(q.shape)  16.3 us
    reduce_sum x1, other arithmetic, together(): jnp.sum(total * scale, 0)  7.09 us
    reduce_max x1, other arithmetic, together(): scale = jnp.exp(high - jnp.max(high, 0))  5.08 us
    unnamed x5, local copies, waits for them, and re-layouts  4.32 us
  transfers between devices with their start and end apart: 1, of which 1 were waited for; matrix products, arithmetic and copies ran while one was open for 0% of the time, Pallas kernels for 0%

commit v1 on v0

v1 whole, which is shorter than its diff:
```python
import functools
import math

import jax
import jax.numpy as jnp
from jax import lax
from jax.experimental import pallas as pl
from jax.experimental.pallas import tpu as pltpu
from jax.sharding import PartitionSpec as P

MESH = pl.DeviceIdType.MESH
SLOTS = 8
LANES = 128
PITCH = 16
AHEAD = 5


def kernel(n, kv, share, scale, q_hbm, k_hbm, v_hbm, o_hbm, q_buf, q_pad, k_buf, v_buf, m_even, m_odd, t_even, t_odd,
           part, stat, got, got_stat, rows, result, q_sem, k_sem, v_sem, send_sem, recv_sem, out_send, out_recv, own_sem):
    sequences, tall, head = k_hbm.shape
    me = lax.axis_index("sp")
    group = tall // 8
    half = tall // 2
    blocks = sequences // n
    power = scale * math.log2(math.e)

    def k_copy(b):
        slot = lax.rem(b, SLOTS)
        return pltpu.make_async_copy(k_hbm.at[b], k_buf.at[slot], k_sem.at[slot])

    def v_copy(b):
        slot = lax.rem(b, SLOTS)
        return pltpu.make_async_copy(v_hbm.at[b], v_buf.at[slot], v_sem.at[slot])

    q_copy = pltpu.make_async_copy(q_hbm, q_buf, q_sem)
    q_copy.start()
    for b in range(SLOTS):
        k_copy(jnp.int32(b)).start()
        v_copy(jnp.int32(b)).start()

    barrier = pltpu.get_barrier_semaphore()
    for d in range(1, n):
        pl.semaphore_signal(barrier, inc=1, device_id={"sp": lax.rem(me + d, n)}, device_id_type=MESH)

    q_copy.wait()

    def spread(b, carry):
        x = q_buf[b].astype(jnp.float32)
        zeros = jnp.zeros((PITCH - share, head), jnp.float32)
        pieces = []
        for h in range(kv):
            pieces += [x[h * share:(h + 1) * share], zeros]
        q_pad[b] = jnp.concatenate(pieces, 0).astype(jnp.bfloat16)
        return carry

    lax.fori_loop(0, sequences, spread, 0)
    pl.semaphore_wait(barrier, n - 1)

    lane = lax.broadcasted_iota(jnp.int32, (8, LANES), 1)
    line = lax.broadcasted_iota(jnp.int32, (8, LANES), 0)
    turn = lax.rem(lane // (2 * PITCH) - lax.rem(line, kv) + kv, kv)
    masks = [turn == w for w in range(kv)]
    lane_row = lax.rem(lax.broadcasted_iota(jnp.int32, (PITCH, LANES), 1), kv)
    keep = [jnp.where(lane_row == h, 1.0, 0.0).astype(jnp.bfloat16) for h in range(kv)]

    def scores(b, m_ref):
        slot = lax.rem(b, SLOTS)
        q = q_pad[b]
        none = jnp.zeros((PITCH, head), jnp.bfloat16)
        for w in range(kv):
            rows_of = []
            for k in range(2 * kv):
                h = (k // 2 - w) % kv
                piece = q[h * PITCH:(h + 1) * PITCH]
                rows_of.append(jnp.concatenate([piece, none] if k % 2 == 0 else [none, piece], 1))
            weights = jnp.concatenate(rows_of, 0)
            keys = jnp.concatenate([k_buf[slot, pl.ds(2 * w * group, group), :], k_buf[slot, pl.ds((2 * w + 1) * group, group), :]], 1)
            s = lax.dot_general(keys, weights, (((1,), (1,)), ((), ())), preferred_element_type=jnp.float32)
            s = s.reshape(group // 8, 8, LANES)
            if w == 0:
                m_ref[...] = s
            else:
                pltpu.store(m_ref, s, mask=jnp.broadcast_to(masks[w][None], s.shape))

    def across(x, op):
        x = op(x, pltpu.roll(x, kv, 0))
        for step in (PITCH, 2 * PITCH, 4 * PITCH):
            x = op(x, pltpu.roll(x, step, 1))
        return x

    def soft(b, m_ref, t_ref):
        s = m_ref[...]
        high = across(jnp.max(s, 0), jnp.maximum)
        p = jnp.exp2((s - high[None]) * power)
        total = across(jnp.sum(p, 0), jnp.add)
        stat[b] = jnp.where(lane < LANES // 2, high, total)
        t_ref[...] = p.reshape(group, LANES).astype(jnp.bfloat16).T

    def mix(b, t_ref):
        slot = lax.rem(b, SLOTS)
        t = t_ref[...]

        def line_of(first):
            columns = []
            for g in range(4):
                w, side = (first + g) // 2, (first + g) % 2
                lines = []
                for h in range(kv):
                    k = 2 * ((h + w) % kv) + side
                    lines.append(t[k * PITCH:(k + 1) * PITCH] * jnp.concatenate([keep[h]] * (group // LANES), 1))
                columns.append(jnp.concatenate(lines, 0))
            return jnp.concatenate(columns, 1)

        left = jnp.concatenate([line_of(0), line_of(4)], 0)
        values = jnp.concatenate([v_buf[slot, pl.ds(0, half), :], v_buf[slot, pl.ds(half, half), :]], 1)
        both = jnp.dot(left, values, preferred_element_type=jnp.float32)
        tall_rows = kv * PITCH
        part[b] = (both[:tall_rows, :head] + both[tall_rows:, head:]).astype(jnp.bfloat16)

    def sends(b):
        i, owner = b // n, lax.rem(b, n)
        to = dict(device_id={"sp": owner}, device_id_type=MESH)
        return (
            pltpu.make_async_remote_copy(src_ref=part.at[b], dst_ref=got.at[i, me], send_sem=send_sem.at[b, 0], recv_sem=recv_sem.at[i, me, 0], **to),
            pltpu.make_async_remote_copy(src_ref=stat.at[b], dst_ref=got_stat.at[i, me], send_sem=send_sem.at[b, 1], recv_sem=recv_sem.at[i, me, 1], **to),
        )

    def send(b):
        @pl.when(lax.rem(b, n) != me)
        def _():
            for copy in sends(b):
                copy.start()

    def arrivals(i, d):
        to = dict(device_id={"sp": d}, device_id_type=MESH)
        return (
            pltpu.make_async_remote_copy(src_ref=part.at[0], dst_ref=got.at[i, d], send_sem=send_sem.at[0, 0], recv_sem=recv_sem.at[i, d, 0], **to),
            pltpu.make_async_remote_copy(src_ref=stat.at[0], dst_ref=got_stat.at[i, d], send_sem=send_sem.at[0, 1], recv_sem=recv_sem.at[i, d, 1], **to),
        )

    def outs(i, d):
        b = i * n + me
        return pltpu.make_async_remote_copy(
            src_ref=result.at[i], dst_ref=o_hbm.at[b], send_sem=out_send.at[i, d], recv_sem=out_recv.at[b],
            device_id={"sp": d}, device_id_type=MESH)

    def own(i):
        return pltpu.make_async_copy(result.at[i], o_hbm.at[i * n + me], own_sem.at[i])

    def together(i):
        b = i * n + me
        got[i, me] = part[b]
        got_stat[i, me] = stat[b]
        for d in range(1, n):
            for copy in arrivals(i, lax.rem(me + d, n)):
                copy.wait_recv()
        stats = [got_stat[i, d] for d in range(n)]
        high = functools.reduce(jnp.maximum, stats)
        factors = [jnp.exp2((x - high) * power) for x in stats]
        total = functools.reduce(jnp.add, [pltpu.roll(x, LANES // 2, 1) * f for x, f in zip(stats, factors)])
        factors = jnp.concatenate([f / total for f in factors] + [jnp.zeros((LANES - 8 * n, LANES), jnp.float32)], 0).T
        for h in range(kv):
            acc = None
            for d in range(n):
                x = got[i, d, pl.ds(h * PITCH, PITCH), :].astype(jnp.float32)
                x = x * factors[:PITCH, 8 * d + h:8 * d + h + 1]
                acc = x if acc is None else acc + x
            rows[pl.ds(h * share, share), :] = acc[:share]
        result[i] = rows[...].astype(jnp.bfloat16)
        own(i).start()
        for d in range(1, n):
            outs(i, lax.rem(me + d, n)).start()

    def step(b, even, a=True, s=True, c=True):
        m_now, m_before = (m_even, m_odd) if even else (m_odd, m_even)
        t_now, t_before = (t_odd, t_even) if even else (t_even, t_odd)
        if a:
            k_copy(b).wait()
        if c:
            v_copy(b - 2).wait()
        if a:
            scores(b, m_now)
        if s:
            soft(b - 1, m_before, t_now)
        if c:
            mix(b - 2, t_before)
        if a:
            @pl.when(b + SLOTS < sequences)
            def _():
                k_copy(b + SLOTS).start()
        if c:
            @pl.when(b - 2 + SLOTS < sequences)
            def _():
                v_copy(b - 2 + SLOTS).start()
            send(b - 2)

    step(jnp.int32(0), True, s=False, c=False)
    step(jnp.int32(1), False, c=False)

    def pair(j, carry):
        b = 2 * j + 2
        step(b, True)

        @pl.when((lax.rem(b - AHEAD - 1, n) == 0) & (b > n + AHEAD))
        def _():
            together((b - AHEAD - 1) // n - 1)

        step(b + 1, False)
        return carry

    lax.fori_loop(0, (sequences - 2) // 2, pair, 0)
    step(jnp.int32(sequences), True, a=False)
    step(jnp.int32(sequences + 1), False, a=False, s=False)
    together(jnp.int32(blocks - 1))

    def finish(b, carry):
        i, owner = b // n, lax.rem(b, n)

        @pl.when(owner != me)
        def _():
            for copy in sends(b):
                copy.wait_send()
            pltpu.make_async_remote_copy(
                src_ref=result.at[i], dst_ref=o_hbm.at[b], send_sem=out_send.at[i, owner], recv_sem=out_recv.at[b],
                device_id={"sp": owner}, device_id_type=MESH).wait_recv()
            outs(i, owner).wait_send()

        @pl.when(owner == me)
        def _():
            own(i).wait()

        return carry

    lax.fori_loop(0, sequences, finish, 0)


def solution(mesh):
    n = mesh.shape["sp"]

    def step(q, k, v):
        sequences, heads, head = q.shape
        tokens, kv = k.shape[1:3]
        share = heads // kv
        tall = tokens * kv
        group = tall // 8
        blocks = sequences // n
        lines = kv * PITCH
        bf16, f32 = jnp.bfloat16, jnp.float32
        anywhere = pl.BlockSpec(memory_space=pl.ANY)
        dma = pltpu.SemaphoreType.DMA
        return pl.pallas_call(
            functools.partial(kernel, n, kv, share, head ** -0.5),
            out_shape=jax.ShapeDtypeStruct(q.shape, bf16),
            in_specs=[anywhere] * 3,
            out_specs=anywhere,
            scratch_shapes=[
                pltpu.VMEM((sequences, heads, head), bf16),
                pltpu.VMEM((sequences, lines, head), bf16),
                pltpu.VMEM((SLOTS, tall, head), bf16),
                pltpu.VMEM((SLOTS, tall, head), bf16),
                pltpu.VMEM((group // 8, 8, LANES), f32),
                pltpu.VMEM((group // 8, 8, LANES), f32),
                pltpu.VMEM((LANES, group), bf16),
                pltpu.VMEM((LANES, group), bf16),
                pltpu.VMEM((sequences, lines, head), bf16),
                pltpu.VMEM((sequences, 8, LANES), f32),
                pltpu.VMEM((blocks, n, lines, head), bf16),
                pltpu.VMEM((blocks, n, 8, LANES), f32),
                pltpu.VMEM((heads, head), f32),
                pltpu.VMEM((blocks, heads, head), bf16),
                dma,
                dma((SLOTS,)),
                dma((SLOTS,)),
                dma((sequences, 2)),
                dma((blocks, n, 2)),
                dma((blocks, n)),
                dma((sequences,)),
                dma((blocks,)),
            ],
            compiler_params=pltpu.CompilerParams(collective_id=0, has_side_effects=True, vmem_limit_bytes=48 * 2 ** 20),
            name="decode",
        )(q, k.reshape(sequences, tall, head), v.reshape(sequences, tall, head))

    return jax.shard_map(
        step,
        mesh=mesh,
        in_specs=(P("dp", None, None), P("dp", "sp", None, None), P("dp", "sp", None, None)),
        out_specs=P("dp", None, None),
        check_vma=False,
    )
```

time: 159 us -> 38.7 us (0.24)
  waiting for transfers between devices: 66.8 us -> 0 us
  Pallas kernels: 0 us -> 36.8 us
  matrix products: 36 us -> 0 us
  local copies, waits for them, and re-layouts: 25.9 us -> 1.74 us
  other arithmetic: 16.8 us -> 0 us
  between operations: 13.5 us -> 0.01 us
    all_gather x1 -> x0, waiting for transfers between devices: 66.7 us -> none  [step(): return together(lax.all_gather(part_of(q, k, v), 'sp')).reshape(q.shape)]
    pallas_call x0 -> x1, Pallas kernels: none -> 36.8 us  [step(): pl.pallas_call(functools.partial(kernel, n, kv, share, head ** (-0.5)), o...]
    dot_general x2 -> x0, matrix products: 36 us -> none  [einsum(): return jnp.einsum(form, a.astype(jnp.float32), b.astype(jnp.float32))]
    all_gather x1 -> x0, local copies, waits for them, and re-layouts: 16.3 us -> none  [step(): return together(lax.all_gather(part_of(q, k, v), 'sp')).reshape(q.shape)]
    reduce_sum x3 -> x0, other arithmetic: 11.1 us -> none  [the longest x1 7.09 us: together(): jnp.sum(total * scale, 0)]
    reduce_max x1 -> x0, other arithmetic: 5.08 us -> none  [together(): scale = jnp.exp(high - jnp.max(high, 0))]
    unnamed x5 -> x3, local copies, waits for them, and re-layouts: 4.32 us -> 1.74 us
    concatenate x1 -> x0, local copies, waits for them, and re-layouts: 2.54 us -> none  [part_of(): jnp.concatenate([seen, jnp.sum(weights, -1, keepdims=True), high], -1)]
  transfers between devices with their start and end apart: 1 -> 0, of which waited for: 1 -> 0; matrix products, arithmetic and copies ran while one was open for 0% -> 0% of each run, Pallas kernels for 0% -> 0%
where the time goes in v1:
time: 38.7 us; the launch traced here: 38.6 us
  Pallas kernels  36.8 us (95%)
  local copies, waits for them, and re-layouts  1.74 us (4%)
    pallas_call x1, Pallas kernels, step(): pl.pallas_call(functools.partial(kernel, n, kv, share, head ** (-0.5)), o...  36.8 us
    unnamed x3, local copies, waits for them, and re-layouts  1.74 us

profile of v1, /device:TPU:113, one launch (start us, length us, event | category | flops | bytes accessed | tf_op | source)
XLA Modules:
  0.0 38.6 jit_solution(10166601232703984713)
XLA Ops:
  0.0 0.0 copy-start
  0.0 1.0 %copy-done = bf16[32,48,128]{2,1,0:T(8,128)(2,1)S(1)} copy-done((bf16[32,48,128]{2,1,0:T(8,128)(2,1)S(1)}, bf16[32,48,128]{2,1,0:T(8,128)(2,1)}, u32[]{:S(2)}) %copy-start) | copy-done | bytes 393240
  1.0 36.8 %decode.1 = bf16[32,48,128]{2,1,0:T(8,128)(2,1)S(1)} custom-call(bf16[32,48,128]{2,1,0:T(8,128)(2,1)S(1)} %copy-done, bf16[32,4096,128]{2,1,0:T(8,128)(2,1)} %bitcast.2, bf16[32,4096,128]{2,1,0:T(8,128)(2,1)} %bitcast.3), custom_call_target="tpu_custom_call" | custom-call | tf_op jit(solution)/shard_map/decode/pallas_call | solution.py:251
  37.8 0.7 %copy.5 = bf16[32,48,128]{2,1,0:T(8,128)(2,1)} copy(bf16[32,48,128]{2,1,0:T(8,128)(2,1)S(1)} %decode.1) | data formatting | bytes 786432
Async XLA Ops:
  0.0 1.0 %copy-start = (bf16[32,48,128]{2,1,0:T(8,128)(2,1)S(1)}, bf16[32,48,128]{2,1,0:T(8,128)(2,1)}, u32[]{:S(2)}) copy-start(bf16[32,48,128]{2,1,0:T(8,128)(2,1)} %q_hbm.1) | copy-start | bytes 1179652

commit v2 on v1

v2 whole, which is shorter than its diff:
```python
import functools
import math

import jax
import jax.numpy as jnp
from jax import lax
from jax.experimental import pallas as pl
from jax.experimental.pallas import tpu as pltpu
from jax.sharding import PartitionSpec as P

MESH = pl.DeviceIdType.MESH
PIECES = 4
SLOTS = 8
LANES = 128
PITCH = 16


def kernel(n, kv, share, scale, q_hbm, k_hbm, v_hbm, o_ref, q_buf, k_buf, v_buf, m_even, m_odd, t_even, t_odd,
           part, stat, got, got_stat, late, late_stat, q_sem, k_sem, v_sem, part_send, stat_send, late_send, late_stat_send,
           part_recv, stat_recv, late_recv, late_stat_recv, out_send, out_recv, pair_send, pair_recv):
    sequences, tall, head = k_hbm.shape
    heads = kv * share
    me = lax.axis_index("sp")
    port = lax.rem(me, 2) == 1
    group = tall // 8
    half = tall // 2
    early = sequences - n
    power = scale * math.log2(math.e)

    def k_copy(b):
        slot = lax.rem(b, SLOTS)
        return pltpu.make_async_copy(k_hbm.at[b], k_buf.at[slot], k_sem.at[slot])

    def v_copy(b):
        slot = lax.rem(b, SLOTS)
        return pltpu.make_async_copy(v_hbm.at[b], v_buf.at[slot], v_sem.at[slot])

    q_copy = pltpu.make_async_copy(q_hbm, q_buf, q_sem)
    q_copy.start()
    for i in range(PIECES):
        rows = pl.ds(i * (tall // PIECES), tall // PIECES)
        pltpu.make_async_copy(k_hbm.at[0, rows, :], k_buf.at[0, rows, :], k_sem.at[0]).start()
    k_copy(jnp.int32(1)).start()
    v_copy(jnp.int32(0)).start()

    barrier = pltpu.get_barrier_semaphore()
    for d in range(1, n):
        pl.semaphore_signal(barrier, inc=1, device_id={"sp": lax.rem(me + d, n)}, device_id_type=MESH)
    q_copy.wait()

    lane = lax.broadcasted_iota(jnp.int32, (8, LANES), 1)
    line = lax.broadcasted_iota(jnp.int32, (8, LANES), 0)
    turn = lax.rem(lane // (2 * PITCH) - lax.rem(line, kv) + kv, kv)
    masks = [turn == w for w in range(kv)]
    once = (lax.rem(lane // PITCH, kv) == line)
    lane_row = lax.rem(lax.broadcasted_iota(jnp.int32, (PITCH, LANES), 1), kv)
    keep = [jnp.where(lane_row == h, 1.0, 0.0).astype(jnp.bfloat16) for h in range(kv)]

    def scores(b, m_ref):
        slot = lax.rem(b, SLOTS)
        x = q_buf[b].astype(jnp.float32)
        spare = jnp.zeros((PITCH - share, head), jnp.float32)
        q = [jnp.concatenate([x[h * share:(h + 1) * share], spare], 0).astype(jnp.bfloat16) for h in range(kv)]
        none = jnp.zeros((PITCH, head), jnp.bfloat16)
        for w in range(kv):
            rows_of = []
            for k in range(2 * kv):
                piece = q[(k // 2 - w) % kv]
                rows_of.append(jnp.concatenate([piece, none] if k % 2 == 0 else [none, piece], 1))
            weights = jnp.concatenate(rows_of, 0)
            keys = jnp.concatenate([k_buf[slot, pl.ds(2 * w * group, group), :], k_buf[slot, pl.ds((2 * w + 1) * group, group), :]], 1)
            s = lax.dot_general(keys, weights, (((1,), (1,)), ((), ())), preferred_element_type=jnp.float32)
            s = s.reshape(group // 8, 8, LANES)
            if w == 0:
                m_ref[...] = s
            else:
                pltpu.store(m_ref.at[pl.ds(0, group // 8)], s, mask=jnp.broadcast_to(masks[w][None], s.shape))

    def across(x, op):
        x = op(x, pltpu.roll(x, kv, 0))
        for step in (PITCH, 2 * PITCH, 4 * PITCH):
            x = op(x, pltpu.roll(x, step, 1))
        return x

    def soft(b, m_ref, t_ref):
        s = m_ref[...]
        high = across(jnp.max(s, 0), jnp.maximum)
        p = jnp.exp2((s - high[None]) * power)
        total = across(jnp.sum(p, 0), jnp.add)
        stat[b] = jnp.sum(jnp.where(once, jnp.where(lane < LANES // 2, high, total), 0.0), 0, keepdims=True)
        t_ref[...] = p.reshape(group, LANES).astype(jnp.bfloat16).T

    def compact(x):
        return jnp.concatenate([x[h * PITCH:h * PITCH + share] for h in range(kv)], 0)

    def mix(b, t_ref):
        slot = lax.rem(b, SLOTS)
        t = t_ref[...]

        def line_of(first):
            columns = []
            for g in range(4):
                w, side = (first + g) // 2, (first + g) % 2
                lines = []
                for h in range(kv):
                    k = 2 * ((h + w) % kv) + side
                    lines.append(t[k * PITCH:(k + 1) * PITCH] * jnp.concatenate([keep[h]] * (group // LANES), 1))
                columns.append(jnp.concatenate(lines, 0))
            return jnp.concatenate(columns, 1)

        left = jnp.concatenate([line_of(0), line_of(4)], 0)
        values = jnp.concatenate([v_buf[slot, pl.ds(0, half), :], v_buf[slot, pl.ds(half, half), :]], 1)
        both = jnp.dot(left, values, preferred_element_type=jnp.float32)
        high = kv * PITCH
        part[b] = compact(both[:high, :head] + both[high:, head:]).astype(jnp.bfloat16)

    def remote(src, dst, send_sem, recv_sem, to):
        return pltpu.make_async_remote_copy(src_ref=src, dst_ref=dst, send_sem=send_sem, recv_sem=recv_sem, device_id={"sp": to}, device_id_type=MESH)

    def send_early(b):
        @pl.when((b < early) & (lax.rem(b, n) != me))
        def _():
            k, owner = b // n, lax.rem(b, n)
            remote(stat.at[b], got_stat.at[k, me], stat_send, stat_recv.at[k, me], owner).start()
            remote(part.at[b], got.at[k, me], part_send, part_recv.at[k, me], owner).start()

    def send_late(what, there, send_sem, recv_sem, first, count, group_index):
        for to in range(1, n, 2):
            @pl.when(me != to)
            def _():
                remote(what.at[pl.ds(early + first, count)], there.at[me, pl.ds(first, count)], send_sem, recv_sem.at[group_index, me], jnp.int32(to)).start()

    def late_part(first, count, group_index):
        send_late(part, late, late_send, late_recv, first, count, group_index)

    def late_stats(first, count, group_index):
        send_late(stat, late_stat, late_stat_send, late_stat_recv, first, count, group_index)

    def factors(rows):
        out = []
        for list_of in rows:
            x = jnp.concatenate(list_of, 0)
            f = jnp.exp2((x - jnp.max(x, 0, keepdims=True)) * power)
            total = jnp.sum(pltpu.roll(x, LANES // 2, 1) * f, 0, keepdims=True)
            out.append(f / total)
        if len(rows) * n < LANES:
            out.append(jnp.zeros((LANES - len(rows) * n, LANES), jnp.float32))
        return compact(jnp.concatenate(out, 0).T)

    def put_together(parts, f, i):
        acc = None
        for d, x in enumerate(parts):
            x = x.astype(jnp.float32) * f[:, n * i + d:n * i + d + 1]
            acc = x if acc is None else acc + x
        return acc.astype(jnp.bfloat16)

    def together(k):
        b = k * n + me
        got[k, me] = part[b]
        got_stat[k, me] = stat[b]
        for d in range(1, n):
            other = lax.rem(me + d, n)
            remote(stat.at[0], got_stat.at[k, other], stat_send, stat_recv.at[k, other], other).wait_recv()
            remote(part.at[0], got.at[k, other], part_send, part_recv.at[k, other], other).wait_recv()
        f = factors([[got_stat[k, d] for d in range(n)]])
        o_ref[b] = put_together([got[k, d] for d in range(n)], f, 0)
        for d in range(1, n):
            remote(o_ref.at[b], o_ref.at[b], out_send, out_recv, lax.rem(me + d, n)).start()

    def late_wait(what, there, send_sem, recv_sem, first, count, group_index):
        there[me, pl.ds(first, count)] = what[pl.ds(early + first, count)]
        for d in range(1, n):
            other = lax.rem(me + d, n)
            remote(what.at[pl.ds(0, count)], there.at[other, pl.ds(first, count)], send_sem, recv_sem.at[group_index, other], other).wait_recv()

    def late_factors(first, count):
        return factors([[late_stat[d, first + i] for d in range(n)] for i in range(count)])

    def late_together(first, count, group_index, f, at):
        late_wait(part, late, late_send, late_recv, first, count, group_index)
        for i in range(count):
            o_ref[early + first + i] = put_together([late[d, first + i] for d in range(n)], f, at + i)
        rows = o_ref.at[pl.ds(early + first, count)]
        remote(rows, rows, pair_send, pair_recv, me - 1).start()

    def step(b, even, a=True, s=True, c=True):
        m_now, m_before = (m_even, m_odd) if even else (m_odd, m_even)
        t_now, t_before = (t_odd, t_even) if even else (t_even, t_odd)
        if c:
            if a:
                k_copy(b).wait()
            v_copy(b - 2).wait()
        if a:
            scores(b, m_now)
        if s:
            soft(b - 1, m_before, t_now)
        if c:
            mix(b - 2, t_before)
        if c:
            @pl.when(b + SLOTS < sequences)
            def _():
                k_copy(b + SLOTS).start()

            @pl.when(b - 2 + SLOTS < sequences)
            def _():
                v_copy(b - 2 + SLOTS).start()

    def more(ks, vs):
        for i in ks:
            k_copy(jnp.int32(i)).start()
        for i in vs:
            v_copy(jnp.int32(i)).start()

    k_copy(jnp.int32(0)).wait()
    more((2, 3), (1,))
    step(jnp.int32(0), True, s=False, c=False)
    k_copy(jnp.int32(1)).wait()
    more((4, 5), (2, 3))
    step(jnp.int32(1), False, c=False)
    more((6, 7, 8, 9), (4, 5, 6, 7))
    pl.semaphore_wait(barrier, n - 1)

    def pair(j, carry):
        b = 2 * j + 2

        @pl.when((lax.rem(b, n) == 0) & (b > n))
        def _():
            together(b // n - 2)

        step(b, True)
        send_early(b - 2)
        step(b + 1, False)
        send_early(b - 1)

        @pl.when(b - 2 >= early)
        def _():
            first = b - 2 - early
            late_part(first, 2, first // 2)

        @pl.when(b == early + n // 2 + 2)
        def _():
            late_stats(0, n // 2 + 2, 0)

        return carry

    lax.fori_loop(0, (sequences - 2) // 2, pair, 0)
    step(jnp.int32(sequences), True, a=False)
    late_stats(n - 2, 2, 1)
    late_part(n - 2, 1, n // 2 - 1)
    step(jnp.int32(sequences + 1), False, a=False, s=False)
    late_part(n - 1, 1, n // 2)
    together(jnp.int32(early // n - 1))

    mine = early // n
    others = early - mine

    def sent(what, count, sem):
        remote(what.at[pl.ds(0, count)], what.at[pl.ds(0, count)], sem, pair_recv, lax.rem(me + 1, n)).wait_send()

    def early_waits():
        sent(part, others, part_send)
        sent(stat, others, stat_send)
        sent(o_ref, others, out_send)
        remote(o_ref.at[pl.ds(0, others)], o_ref.at[pl.ds(0, others)], pair_send, out_recv, lax.rem(me + 1, n)).wait_recv()

    @pl.when(port)
    def _():
        late_wait(stat, late_stat, late_stat_send, late_stat_recv, 0, n // 2 + 2, 0)
        f = late_factors(0, n // 2 + 2)
        for i in range(n // 2 - 1):
            late_together(2 * i, 2, i, f, 2 * i)
        late_wait(stat, late_stat, late_stat_send, late_stat_recv, n - 2, 2, 1)
        f = late_factors(n - 2, 2)
        late_together(n - 2, 1, n // 2 - 1, f, 0)
        late_together(n - 1, 1, n // 2, f, 1)
        early_waits()
        sent(part, (n // 2 - 1) * n, late_send)
        sent(stat, (n // 2 - 1) * n, late_stat_send)
        sent(o_ref, n, pair_send)

    @pl.when(jnp.logical_not(port))
    def _():
        early_waits()
        sent(part, n // 2 * n, late_send)
        sent(stat, n // 2 * n, late_stat_send)
        rows = o_ref.at[pl.ds(early, n)]
        remote(rows, rows, pair_send, pair_recv, me + 1).wait_recv()


def solution(mesh):
    n = mesh.shape["sp"]

    def step(q, k, v):
        sequences, heads, head = q.shape
        tokens, kv = k.shape[1:3]
        share = heads // kv
        tall = tokens * kv
        group = tall // 8
        blocks = sequences // n - 1
        bf16, f32 = jnp.bfloat16, jnp.float32
        anywhere = pl.BlockSpec(memory_space=pl.ANY)
        dma = pltpu.SemaphoreType.DMA
        return pl.pallas_call(
            functools.partial(kernel, n, kv, share, head ** -0.5),
            out_shape=jax.ShapeDtypeStruct(q.shape, bf16),
            in_specs=[anywhere] * 3,
            out_specs=pl.BlockSpec(memory_space=pltpu.VMEM),
            scratch_shapes=[
                pltpu.VMEM((sequences, heads, head), bf16),
                pltpu.VMEM((SLOTS, tall, head), bf16),
                pltpu.VMEM((SLOTS, tall, head), bf16),
                pltpu.VMEM((group // 8, 8, LANES), f32),
                pltpu.VMEM((group // 8, 8, LANES), f32),
                pltpu.VMEM((LANES, group), bf16),
                pltpu.VMEM((LANES, group), bf16),
                pltpu.VMEM((sequences, heads, head), bf16),
                pltpu.VMEM((sequences, 1, LANES), f32),
                pltpu.VMEM((blocks, n, heads, head), bf16),
                pltpu.VMEM((blocks, n, 1, LANES), f32),
                pltpu.VMEM((n, n, heads, head), bf16),
                pltpu.VMEM((n, n, 1, LANES), f32),
                dma,
                dma((SLOTS,)),
                dma((SLOTS,)),
                dma,
                dma,
                dma,
                dma,
                dma((blocks, n)),
                dma((blocks, n)),
                dma((n // 2 + 1, n)),
                dma((2, n)),
                dma,
                dma,
                dma,
                dma,
            ],
            compiler_params=pltpu.CompilerParams(collective_id=0, has_side_effects=True, vmem_limit_bytes=56_000_000),
            name="decode",
        )(q, k.reshape(sequences, tall, head), v.reshape(sequences, tall, head))

    return jax.shard_map(
        step,
        mesh=mesh,
        in_specs=(P("dp", None, None), P("dp", "sp", None, None), P("dp", "sp", None, None)),
        out_specs=P("dp", None, None),
        check_vma=False,
    )
```

time: 38.7 us -> 33.9 us (0.88)
  Pallas kernels: 36.8 us -> 33.1 us
  local copies, waits for them, and re-layouts: 1.74 us -> 0.75 us
    pallas_call x1, Pallas kernels: 36.8 us -> 33.1 us  [step(): pl.pallas_call(functools.partial(kernel, n, kv, share, head ** (-0.5)), o...]
    unnamed x3 -> x1, local copies, waits for them, and re-layouts: 1.74 us -> 0.75 us
where the time goes in v2:
time: 33.9 us; the launch traced here: 33.8 us
  Pallas kernels  33.1 us (98%)
  local copies, waits for them, and re-layouts  0.75 us (2%)
    pallas_call x1, Pallas kernels, step(): pl.pallas_call(functools.partial(kernel, n, kv, share, head ** (-0.5)), o...  33.1 us
    unnamed x1, local copies, waits for them, and re-layouts  0.75 us

profile of v2, /device:TPU:113, one launch (start us, length us, event | category | flops | bytes accessed | tf_op | source)
XLA Modules:
  0.0 33.8 jit_solution(9136522852216221265)
XLA Ops:
  0.0 33.1 %decode.1 = bf16[32,48,128]{2,1,0:T(8,128)(2,1)S(1)} custom-call(bf16[32,48,128]{2,1,0:T(8,128)(2,1)} %q_hbm.1, bf16[32,4096,128]{2,1,0:T(8,128)(2,1)} %bitcast.2, bf16[32,4096,128]{2,1,0:T(8,128)(2,1)} %bitcast.3), custom_call_target="tpu_custom_call" | custom-call | tf_op jit(solution)/shard_map/decode/pallas_call | solution.py:303
  33.1 0.7 %copy.5 = bf16[32,48,128]{2,1,0:T(8,128)(2,1)} copy(bf16[32,48,128]{2,1,0:T(8,128)(2,1)S(1)} %decode.1) | data formatting | bytes 786432

commit v3 on v2

--- a/solution.py
+++ b/solution.py
@@ -26,6 +26,7 @@
     half = tall // 2
     early = sequences - n
     power = scale * math.log2(math.e)
+    partner = me + 1 - 2 * lax.rem(me, 2)
 
     def k_copy(b):
         slot = lax.rem(b, SLOTS)
@@ -118,17 +119,19 @@
         return pltpu.make_async_remote_copy(src_ref=src, dst_ref=dst, send_sem=send_sem, recv_sem=recv_sem, device_id={"sp": to}, device_id_type=MESH)
 
     def send_early(b):
-        @pl.when((b < early) & (lax.rem(b, n) != me))
-        def _():
-            k, owner = b // n, lax.rem(b, n)
-            remote(stat.at[b], got_stat.at[k, me], stat_send, stat_recv.at[k, me], owner).start()
-            remote(part.at[b], got.at[k, me], part_send, part_recv.at[k, me], owner).start()
+        owner = jnp.where(b < 2 * n, b // 2, b - 2 * n)
+        place = jnp.where(b < 2 * n, lax.rem(b, 2), 2)
+        kept = owner == me
+        to, at = jnp.where(kept, partner, owner), jnp.where(kept, n, me)
+        remote(stat.at[b], got_stat.at[at, place], stat_send, stat_recv.at[place], to).start()
+        remote(part.at[b], got.at[at, place], part_send, part_recv.at[place], to).start()
 
     def send_late(what, there, send_sem, recv_sem, first, count, group_index):
-        for to in range(1, n, 2):
-            @pl.when(me != to)
-            def _():
-                remote(what.at[pl.ds(early + first, count)], there.at[me, pl.ds(first, count)], send_sem, recv_sem.at[group_index, me], jnp.int32(to)).start()
+        for r in range(n // 2):
+            to = lax.rem(me // 2 + r, n // 2) * 2 + 1
+            if r == 0:
+                to = jnp.where(port, partner, to)
+            remote(what.at[pl.ds(early + first, count)], there.at[me, pl.ds(first, count)], send_sem, recv_sem.at[group_index, me], to).start()
 
     def late_part(first, count, group_index):
         send_late(part, late, late_send, late_recv, first, count, group_index)
@@ -154,18 +157,21 @@
             acc = x if acc is None else acc + x
         return acc.astype(jnp.bfloat16)
 
-    def together(k):
-        b = k * n + me
-        got[k, me] = part[b]
-        got_stat[k, me] = stat[b]
+    def arrived(array, count, sem):
+        remote(array.at[pl.ds(0, count)], array.at[pl.ds(0, count)], out_send, sem, partner).wait_recv()
+
+    def together(place, count, first):
+        for i in range(count):
+            arrived(stat, n, stat_recv.at[place + i])
+            arrived(part, n, part_recv.at[place + i])
+            got[me, place + i] = part[first + i]
+            got_stat[me, place + i] = stat[first + i]
+        f = factors([[got_stat[d, place + i] for d in range(n)] for i in range(count)])
+        for i in range(count):
+            o_ref[first + i] = put_together([got[d, place + i] for d in range(n)], f, i)
+        rows = o_ref.at[pl.ds(first, count)]
         for d in range(1, n):
-            other = lax.rem(me + d, n)
-            remote(stat.at[0], got_stat.at[k, other], stat_send, stat_recv.at[k, other], other).wait_recv()
-            remote(part.at[0], got.at[k, other], part_send, part_recv.at[k, other], other).wait_recv()
-        f = factors([[got_stat[k, d] for d in range(n)]])
-        o_ref[b] = put_together([got[k, d] for d in range(n)], f, 0)
-        for d in range(1, n):
-            remote(o_ref.at[b], o_ref.at[b], out_send, out_recv, lax.rem(me + d, n)).start()
+            remote(rows, rows, out_send, out_recv, lax.rem(me + d, n)).start()
 
     def late_wait(what, there, send_sem, recv_sem, first, count, group_index):
         there[me, pl.ds(first, count)] = what[pl.ds(early + first, count)]
@@ -173,6 +179,9 @@
             other = lax.rem(me + d, n)
             remote(what.at[pl.ds(0, count)], there.at[other, pl.ds(first, count)], send_sem, recv_sem.at[group_index, other], other).wait_recv()
 
+    def spared(what, there, send_sem, recv_sem, first, count, group_index):
+        remote(what.at[pl.ds(0, count)], there.at[partner, pl.ds(first, count)], send_sem, recv_sem.at[group_index, partner], partner).wait_recv()
+
     def late_factors(first, count):
         return factors([[late_stat[d, first + i] for d in range(n)] for i in range(count)])
 
@@ -181,9 +190,9 @@
         for i in range(count):
             o_ref[early + first + i] = put_together([late[d, first + i] for d in range(n)], f, at + i)
         rows = o_ref.at[pl.ds(early + first, count)]
-        remote(rows, rows, pair_send, pair_recv, me - 1).start()
-
-    def step(b, even, a=True, s=True, c=True):
+        remote(rows, rows, pair_send, pair_recv, partner).start()
+
+    def step(b, even, a=True, s=True, c=True, more=True, after=None):
         m_now, m_before = (m_even, m_odd) if even else (m_odd, m_even)
         t_now, t_before = (t_odd, t_even) if even else (t_even, t_odd)
         if c:
@@ -196,14 +205,14 @@
             soft(b - 1, m_before, t_now)
         if c:
             mix(b - 2, t_before)
-        if c:
+        if after is not None:
+            after()
+        if c and more:
             @pl.when(b + SLOTS < sequences)
             def _():
                 k_copy(b + SLOTS).start()
 
-            @pl.when(b - 2 + SLOTS < sequences)
-            def _():
-                v_copy(b - 2 + SLOTS).start()
+            v_copy(b - 2 + SLOTS).start()
 
     def more(ks, vs):
         for i in ks:
@@ -223,68 +232,71 @@
     def pair(j, carry):
         b = 2 * j + 2
 
-        @pl.when((lax.rem(b, n) == 0) & (b > n))
+        @pl.when(b == early)
         def _():
-            together(b // n - 2)
-
-        step(b, True)
-        send_early(b - 2)
-        step(b + 1, False)
-        send_early(b - 1)
-
-        @pl.when(b - 2 >= early)
-        def _():
-            first = b - 2 - early
-            late_part(first, 2, first // 2)
-
-        @pl.when(b == early + n // 2 + 2)
-        def _():
-            late_stats(0, n // 2 + 2, 0)
-
+            together(0, 2, 2 * me)
+
+        step(b, True, after=lambda: send_early(b - 2))
+        step(b + 1, False, after=lambda: send_early(b - 1))
         return carry
 
-    lax.fori_loop(0, (sequences - 2) // 2, pair, 0)
-    step(jnp.int32(sequences), True, a=False)
-    late_stats(n - 2, 2, 1)
-    late_part(n - 2, 1, n // 2 - 1)
-    step(jnp.int32(sequences + 1), False, a=False, s=False)
-    late_part(n - 1, 1, n // 2)
-    together(jnp.int32(early // n - 1))
+    lax.fori_loop(0, early // 2, pair, 0)
+
+    def late_pair(j, carry):
+        b = early + 2 + 2 * j
+        step(b, True, more=False)
+        step(b + 1, False, more=False, after=lambda: late_part(2 * j, 2, j))
+        return carry
+
+    lax.fori_loop(0, n // 2 - 1, late_pair, 0)
+    late_stats(0, n - 1, 0)
+    step(jnp.int32(sequences), True, a=False, more=False, after=lambda: (late_stats(n - 1, 1, 1), late_part(n - 2, 1, n // 2 - 1)))
+    step(jnp.int32(sequences + 1), False, a=False, s=False, more=False, after=lambda: late_part(n - 1, 1, n // 2))
+    together(2, 1, 2 * n + me)
 
     mine = early // n
     others = early - mine
 
     def sent(what, count, sem):
-        remote(what.at[pl.ds(0, count)], what.at[pl.ds(0, count)], sem, pair_recv, lax.rem(me + 1, n)).wait_send()
+        remote(what.at[pl.ds(0, count)], what.at[pl.ds(0, count)], sem, pair_recv, partner).wait_send()
 
     def early_waits():
-        sent(part, others, part_send)
-        sent(stat, others, stat_send)
+        sent(part, early, part_send)
+        sent(stat, early, stat_send)
         sent(o_ref, others, out_send)
-        remote(o_ref.at[pl.ds(0, others)], o_ref.at[pl.ds(0, others)], pair_send, out_recv, lax.rem(me + 1, n)).wait_recv()
+        arrived(o_ref, others, out_recv)
+
+    def late_waits():
+        for _ in range(n // 2):
+            sent(part, n, late_send)
+            sent(stat, n, late_stat_send)
 
     @pl.when(port)
     def _():
-        late_wait(stat, late_stat, late_stat_send, late_stat_recv, 0, n // 2 + 2, 0)
-        f = late_factors(0, n // 2 + 2)
+        late_wait(stat, late_stat, late_stat_send, late_stat_recv, 0, n - 1, 0)
+        f = late_factors(0, n - 1)
         for i in range(n // 2 - 1):
             late_together(2 * i, 2, i, f, 2 * i)
-        late_wait(stat, late_stat, late_stat_send, late_stat_recv, n - 2, 2, 1)
-        f = late_factors(n - 2, 2)
-        late_together(n - 2, 1, n // 2 - 1, f, 0)
-        late_together(n - 1, 1, n // 2, f, 1)
+        late_together(n - 2, 1, n // 2 - 1, f, n - 2)
+        late_wait(stat, late_stat, late_stat_send, late_stat_recv, n - 1, 1, 1)
+        f = late_factors(n - 1, 1)
+        late_together(n - 1, 1, n // 2, f, 0)
         early_waits()
-        sent(part, (n // 2 - 1) * n, late_send)
-        sent(stat, (n // 2 - 1) * n, late_stat_send)
+        late_waits()
         sent(o_ref, n, pair_send)
 
     @pl.when(jnp.logical_not(port))
     def _():
         early_waits()
-        sent(part, n // 2 * n, late_send)
-        sent(stat, n // 2 * n, late_stat_send)
+        late_waits()
+        for first, count, i in ((0, n - 1, 0), (n - 1, 1, 1)):
+            spared(stat, late_stat, late_stat_send, late_stat_recv, first, count, i)
+        for i in range(n // 2 - 1):
+            spared(part, late, late_send, late_recv, 2 * i, 2, i)
+        spared(part, late, late_send, late_recv, n - 2, 1, n // 2 - 1)
+        spared(part, late, late_send, late_recv, n - 1, 1, n // 2)
         rows = o_ref.at[pl.ds(early, n)]
-        remote(rows, rows, pair_send, pair_recv, me + 1).wait_recv()
+        remote(rows, rows, pair_send, pair_recv, partner).wait_recv()
 
 
 def solution(mesh):
@@ -296,7 +308,6 @@
         share = heads // kv
         tall = tokens * kv
         group = tall // 8
-        blocks = sequences // n - 1
         bf16, f32 = jnp.bfloat16, jnp.float32
         anywhere = pl.BlockSpec(memory_space=pl.ANY)
         dma = pltpu.SemaphoreType.DMA
@@ -315,8 +326,8 @@
                 pltpu.VMEM((LANES, group), bf16),
                 pltpu.VMEM((sequences, heads, head), bf16),
                 pltpu.VMEM((sequences, 1, LANES), f32),
-                pltpu.VMEM((blocks, n, heads, head), bf16),
-                pltpu.VMEM((blocks, n, 1, LANES), f32),
+                pltpu.VMEM((n + 1, 3, heads, head), bf16),
+                pltpu.VMEM((n + 1, 3, 1, LANES), f32),
                 pltpu.VMEM((n, n, heads, head), bf16),
                 pltpu.VMEM((n, n, 1, LANES), f32),
                 dma,
@@ -326,8 +337,8 @@
                 dma,
                 dma,
                 dma,
-                dma((blocks, n)),
-                dma((blocks, n)),
+                dma((3,)),
+                dma((3,)),
                 dma((n // 2 + 1, n)),
                 dma((2, n)),
                 dma,

time: 33.9 us -> 32.8 us (0.968)
  Pallas kernels: 33.1 us -> 31.9 us
    pallas_call x1, Pallas kernels: 33.1 us -> 31.9 us  [step(): pl.pallas_call(functools.partial(kernel, n, kv, share, head ** (-0.5)), o...]
where the time goes in v3:
time: 32.8 us; the launch traced here: 32.7 us
  Pallas kernels  31.9 us (97%)
  local copies, waits for them, and re-layouts  0.75 us (2%)
    pallas_call x1, Pallas kernels, step(): pl.pallas_call(functools.partial(kernel, n, kv, share, head ** (-0.5)), o...  31.9 us
    unnamed x1, local copies, waits for them, and re-layouts  0.75 us

profile of v3, /device:TPU:113, one launch (start us, length us, event | category | flops | bytes accessed | tf_op | source)
XLA Modules:
  0.0 32.7 jit_solution(11403483114394101037)
XLA Ops:
  0.0 31.9 %decode.1 = bf16[32,48,128]{2,1,0:T(8,128)(2,1)S(1)} custom-call(bf16[32,48,128]{2,1,0:T(8,128)(2,1)} %q_hbm.1, bf16[32,4096,128]{2,1,0:T(8,128)(2,1)} %bitcast.2, bf16[32,4096,128]{2,1,0:T(8,128)(2,1)} %bitcast.3), custom_call_target="tpu_custom_call" | custom-call | tf_op jit(solution)/shard_map/decode/pallas_call | solution.py:314
  31.9 0.7 %copy.5 = bf16[32,48,128]{2,1,0:T(8,128)(2,1)} copy(bf16[32,48,128]{2,1,0:T(8,128)(2,1)S(1)} %decode.1) | data formatting | bytes 786432

commit v4 on v3

--- a/solution.py
+++ b/solution.py
@@ -10,6 +10,7 @@
 
 MESH = pl.DeviceIdType.MESH
 PIECES = 4
+LAG = 8
 SLOTS = 8
 LANES = 128
 PITCH = 16
@@ -17,7 +18,7 @@
 
 def kernel(n, kv, share, scale, q_hbm, k_hbm, v_hbm, o_ref, q_buf, k_buf, v_buf, m_even, m_odd, t_even, t_odd,
            part, stat, got, got_stat, late, late_stat, q_sem, k_sem, v_sem, part_send, stat_send, late_send, late_stat_send,
-           part_recv, stat_recv, late_recv, late_stat_recv, out_send, out_recv, pair_send, pair_recv):
+           part_recv, stat_recv, late_recv, late_stat_recv, out_send, out_recv, hand_send, hand_recv, pair_send, pair_recv):
     sequences, tall, head = k_hbm.shape
     heads = kv * share
     me = lax.axis_index("sp")
@@ -119,12 +120,13 @@
         return pltpu.make_async_remote_copy(src_ref=src, dst_ref=dst, send_sem=send_sem, recv_sem=recv_sem, device_id={"sp": to}, device_id_type=MESH)
 
     def send_early(b):
-        owner = jnp.where(b < 2 * n, b // 2, b - 2 * n)
-        place = jnp.where(b < 2 * n, lax.rem(b, 2), 2)
+        k = b // n
+        owner = lax.rem(b, n) + jnp.where(k == 1, 0, 1)
         kept = owner == me
         to, at = jnp.where(kept, partner, owner), jnp.where(kept, n, me)
-        remote(stat.at[b], got_stat.at[at, place], stat_send, stat_recv.at[place], to).start()
-        remote(part.at[b], got.at[at, place], part_send, part_recv.at[place], to).start()
+        pair_of, places = pl.ds(b, 2), pl.ds(2 * k, 2)
+        remote(stat.at[pair_of], got_stat.at[at, places], stat_send, stat_recv.at[k], to).start()
+        remote(part.at[pair_of], got.at[at, places], part_send, part_recv.at[k], to).start()
 
     def send_late(what, there, send_sem, recv_sem, first, count, group_index):
         for r in range(n // 2):
@@ -160,18 +162,28 @@
     def arrived(array, count, sem):
         remote(array.at[pl.ds(0, count)], array.at[pl.ds(0, count)], out_send, sem, partner).wait_recv()
 
-    def together(place, count, first):
-        for i in range(count):
-            arrived(stat, n, stat_recv.at[place + i])
-            arrived(part, n, part_recv.at[place + i])
-            got[me, place + i] = part[first + i]
-            got_stat[me, place + i] = stat[first + i]
-        f = factors([[got_stat[d, place + i] for d in range(n)] for i in range(count)])
-        for i in range(count):
-            o_ref[first + i] = put_together([got[d, place + i] for d in range(n)], f, i)
-        rows = o_ref.at[pl.ds(first, count)]
-        for d in range(1, n):
-            remote(rows, rows, out_send, out_recv, lax.rem(me + d, n)).start()
+    def come(k, count):
+        arrived(stat, count, stat_recv.at[k])
+        arrived(part, count, part_recv.at[k])
+
+    def together(k):
+        first = k * n + me - lax.rem(me, 2)
+        places = range(2 * k, 2 * k + 2)
+        come(k, 2 * (n - 1))
+        for i, place in enumerate(places):
+            got[me, place] = part[first + i]
+            got_stat[me, place] = stat[first + i]
+        f = factors([[got_stat[d, place] for d in range(n)] for place in places])
+        for i, place in enumerate(places):
+            o_ref[first + i] = put_together([got[d, place] for d in range(n)], f, i)
+        rows = o_ref.at[pl.ds(first, 2)]
+        for d in range(2, n, 2):
+            remote(rows, rows, out_send, out_recv.at[k], lax.rem(me + d, n)).start()
+
+    def hand_on(k):
+        arrived(o_ref, n - 2, out_recv.at[k])
+        rows = o_ref.at[pl.ds(k * n, n)]
+        remote(rows, rows, hand_send, hand_recv, partner).start()
 
     def late_wait(what, there, send_sem, recv_sem, first, count, group_index):
         there[me, pl.ds(first, count)] = what[pl.ds(early + first, count)]
@@ -192,7 +204,7 @@
         rows = o_ref.at[pl.ds(early + first, count)]
         remote(rows, rows, pair_send, pair_recv, partner).start()
 
-    def step(b, even, a=True, s=True, c=True, more=True, after=None):
+    def step(b, even, a=True, s=True, c=True, more=True, between=None, after=None):
         m_now, m_before = (m_even, m_odd) if even else (m_odd, m_even)
         t_now, t_before = (t_odd, t_even) if even else (t_even, t_odd)
         if c:
@@ -203,6 +215,8 @@
             scores(b, m_now)
         if s:
             soft(b - 1, m_before, t_now)
+        if between is not None:
+            between()
         if c:
             mix(b - 2, t_before)
         if after is not None:
@@ -232,39 +246,38 @@
     def pair(j, carry):
         b = 2 * j + 2
 
-        @pl.when(b == early)
+        @pl.when(port & (b == n + LAG))
         def _():
-            together(0, 2, 2 * me)
-
-        step(b, True, after=lambda: send_early(b - 2))
-        step(b + 1, False, after=lambda: send_early(b - 1))
+            together(0)
+
+        @pl.when(jnp.logical_not(port) & (b == 2 * n + LAG))
+        def _():
+            together(1)
+
+        step(b, True)
+        step(b + 1, False, after=lambda: send_early(b - 2))
         return carry
 
     lax.fori_loop(0, early // 2, pair, 0)
 
-    def late_pair(j, carry):
-        b = early + 2 + 2 * j
-        step(b, True, more=False)
-        step(b + 1, False, more=False, after=lambda: late_part(2 * j, 2, j))
-        return carry
-
-    lax.fori_loop(0, n // 2 - 1, late_pair, 0)
-    late_stats(0, n - 1, 0)
-    step(jnp.int32(sequences), True, a=False, more=False, after=lambda: (late_stats(n - 1, 1, 1), late_part(n - 2, 1, n // 2 - 1)))
+    b = jnp.int32(early + 2)
+    for i in range(n - 2):
+        between = (lambda: late_stats(0, n - 1, 0)) if i == n - 3 else None
+        after = (lambda: late_part(i - 1, 2, i // 2)) if i % 2 == 1 else None
+        step(b + i, i % 2 == 0, more=False, between=between, after=after)
+    step(jnp.int32(sequences), True, a=False, more=False, between=lambda: late_stats(n - 1, 1, 1), after=lambda: late_part(n - 2, 1, n // 2 - 1))
     step(jnp.int32(sequences + 1), False, a=False, s=False, more=False, after=lambda: late_part(n - 1, 1, n // 2))
-    together(2, 1, 2 * n + me)
-
-    mine = early // n
-    others = early - mine
+
 
     def sent(what, count, sem):
         remote(what.at[pl.ds(0, count)], what.at[pl.ds(0, count)], sem, pair_recv, partner).wait_send()
 
-    def early_waits():
+    def early_waits(handed):
         sent(part, early, part_send)
         sent(stat, early, stat_send)
-        sent(o_ref, others, out_send)
-        arrived(o_ref, others, out_recv)
+        sent(o_ref, n - 2, out_send)
+        sent(o_ref, n, hand_send)
+        arrived(o_ref, handed, hand_recv)
 
     def late_waits():
         for _ in range(n // 2):
@@ -273,6 +286,9 @@
 
     @pl.when(port)
     def _():
+        hand_on(0)
+        come(1, 2)
+        together(2)
         late_wait(stat, late_stat, late_stat_send, late_stat_recv, 0, n - 1, 0)
         f = late_factors(0, n - 1)
         for i in range(n // 2 - 1):
@@ -281,13 +297,18 @@
         late_wait(stat, late_stat, late_stat_send, late_stat_recv, n - 1, 1, 1)
         f = late_factors(n - 1, 1)
         late_together(n - 1, 1, n // 2, f, 0)
-        early_waits()
+        hand_on(2)
+        early_waits(n)
         late_waits()
+        sent(o_ref, n - 2, out_send)
+        sent(o_ref, n, hand_send)
         sent(o_ref, n, pair_send)
 
     @pl.when(jnp.logical_not(port))
     def _():
-        early_waits()
+        hand_on(1)
+        come(0, 2)
+        come(2, 2)
         late_waits()
         for first, count, i in ((0, n - 1, 0), (n - 1, 1, 1)):
             spared(stat, late_stat, late_stat_send, late_stat_recv, first, count, i)
@@ -295,8 +316,8 @@
             spared(part, late, late_send, late_recv, 2 * i, 2, i)
         spared(part, late, late_send, late_recv, n - 2, 1, n // 2 - 1)
         spared(part, late, late_send, late_recv, n - 1, 1, n // 2)
-        rows = o_ref.at[pl.ds(early, n)]
-        remote(rows, rows, pair_send, pair_recv, partner).wait_recv()
+        early_waits(2 * n)
+        arrived(o_ref, n, pair_recv)
 
 
 def solution(mesh):
@@ -326,8 +347,8 @@
                 pltpu.VMEM((LANES, group), bf16),
                 pltpu.VMEM((sequences, heads, head), bf16),
                 pltpu.VMEM((sequences, 1, LANES), f32),
-                pltpu.VMEM((n + 1, 3, heads, head), bf16),
-                pltpu.VMEM((n + 1, 3, 1, LANES), f32),
+                pltpu.VMEM((n + 1, 6, heads, head), bf16),
+                pltpu.VMEM((n + 1, 6, 1, LANES), f32),
                 pltpu.VMEM((n, n, heads, head), bf16),
                 pltpu.VMEM((n, n, 1, LANES), f32),
                 dma,
@@ -341,6 +362,8 @@
                 dma((3,)),
                 dma((n // 2 + 1, n)),
                 dma((2, n)),
+                dma,
+                dma((3,)),
                 dma,
                 dma,
                 dma,

time: 32.8 us -> 32.7 us (level)
  no operation moved by 1% of the time
where the time goes in v4:
time: 32.7 us; the launch traced here: 32.6 us
  Pallas kernels  31.8 us (97%)
  local copies, waits for them, and re-layouts  0.75 us (2%)
    pallas_call x1, Pallas kernels, step(): pl.pallas_call(functools.partial(kernel, n, kv, share, head ** (-0.5)), o...  31.8 us
    unnamed x1, local copies, waits for them, and re-layouts  0.75 us

profile of v4, /device:TPU:113, one launch (start us, length us, event | category | flops | bytes accessed | tf_op | source)
XLA Modules:
  0.0 32.6 jit_solution(7172656460147086885)
XLA Ops:
  0.0 31.8 %decode.1 = bf16[32,48,128]{2,1,0:T(8,128)(2,1)S(1)} custom-call(bf16[32,48,128]{2,1,0:T(8,128)(2,1)} %q_hbm.1, bf16[32,4096,128]{2,1,0:T(8,128)(2,1)} %bitcast.2, bf16[32,4096,128]{2,1,0:T(8,128)(2,1)} %bitcast.3), custom_call_target="tpu_custom_call" | custom-call | tf_op jit(solution)/shard_map/decode/pallas_call | solution.py:335
  31.8 0.7 %copy.5 = bf16[32,48,128]{2,1,0:T(8,128)(2,1)} copy(bf16[32,48,128]{2,1,0:T(8,128)(2,1)S(1)} %decode.1) | data formatting | bytes 786432

commit v5 on v4

--- a/solution.py
+++ b/solution.py
@@ -58,6 +58,10 @@
     lane_row = lax.rem(lax.broadcasted_iota(jnp.int32, (PITCH, LANES), 1), kv)
     keep = [jnp.where(lane_row == h, 1.0, 0.0).astype(jnp.bfloat16) for h in range(kv)]
 
+    def abreast(x):
+        x = x.reshape(x.shape[0] // (2 * PITCH), 2, PITCH, head)
+        return jnp.concatenate([x[:, side].reshape(-1, head) for side in range(2)], 1)
+
     def scores(b, m_ref):
         slot = lax.rem(b, SLOTS)
         x = q_buf[b].astype(jnp.float32)
@@ -70,7 +74,7 @@
                 piece = q[(k // 2 - w) % kv]
                 rows_of.append(jnp.concatenate([piece, none] if k % 2 == 0 else [none, piece], 1))
             weights = jnp.concatenate(rows_of, 0)
-            keys = jnp.concatenate([k_buf[slot, pl.ds(2 * w * group, group), :], k_buf[slot, pl.ds((2 * w + 1) * group, group), :]], 1)
+            keys = abreast(k_buf[slot, pl.ds(2 * w * group, 2 * group), :])
             s = lax.dot_general(keys, weights, (((1,), (1,)), ((), ())), preferred_element_type=jnp.float32)
             s = s.reshape(group // 8, 8, LANES)
             if w == 0:
@@ -99,10 +103,9 @@
         slot = lax.rem(b, SLOTS)
         t = t_ref[...]
 
-        def line_of(first):
+        def line_of(side):
             columns = []
-            for g in range(4):
-                w, side = (first + g) // 2, (first + g) % 2
+            for w in range(kv):
                 lines = []
                 for h in range(kv):
                     k = 2 * ((h + w) % kv) + side
@@ -110,8 +113,8 @@
                 columns.append(jnp.concatenate(lines, 0))
             return jnp.concatenate(columns, 1)
 
-        left = jnp.concatenate([line_of(0), line_of(4)], 0)
-        values = jnp.concatenate([v_buf[slot, pl.ds(0, half), :], v_buf[slot, pl.ds(half, half), :]], 1)
+        left = jnp.concatenate([line_of(0), line_of(1)], 0)
+        values = abreast(v_buf[slot])
         both = jnp.dot(left, values, preferred_element_type=jnp.float32)
         high = kv * PITCH
         part[b] = compact(both[:high, :head] + both[high:, head:]).astype(jnp.bfloat16)

time: 32.7 us -> 32.7 us (level)
  no operation moved by 1% of the time
where the time goes in v5:
time: 32.7 us; the launch traced here: 32.6 us
  Pallas kernels  31.8 us (97%)
  local copies, waits for them, and re-layouts  0.75 us (2%)
    pallas_call x1, Pallas kernels, step(): pl.pallas_call(functools.partial(kernel, n, kv, share, head ** (-0.5)), o...  31.8 us
    unnamed x1, local copies, waits for them, and re-layouts  0.75 us

profile of v5, /device:TPU:113, one launch (start us, length us, event | category | flops | bytes accessed | tf_op | source)
XLA Modules:
  0.0 32.6 jit_solution(2121667855066753308)
XLA Ops:
  0.0 31.8 %decode.1 = bf16[32,48,128]{2,1,0:T(8,128)(2,1)S(1)} custom-call(bf16[32,48,128]{2,1,0:T(8,128)(2,1)} %q_hbm.1, bf16[32,4096,128]{2,1,0:T(8,128)(2,1)} %bitcast.2, bf16[32,4096,128]{2,1,0:T(8,128)(2,1)} %bitcast.3), custom_call_target="tpu_custom_call" | custom-call | tf_op jit(solution)/shard_map/decode/pallas_call | solution.py:338
  31.8 0.7 %copy.5 = bf16[32,48,128]{2,1,0:T(8,128)(2,1)} copy(bf16[32,48,128]{2,1,0:T(8,128)(2,1)S(1)} %decode.1) | data formatting | bytes 786432
